TPU v7x, 32 devices: a whole 2x2x4 slice. The times are simulated.
32 devices in a mesh: parts: 2 (over x), rows: 16 (over z, y, core).
Axes of the slice: x: 2, y: 2, z: 4, core: 2. Of those that a mesh axis runs over, the one named last changes fastest.
Arguments:
- pair: bfloat16 [64, 32, 128], P(('parts', 'rows')), parts along dimension 0, may hold values from -16 to 16
- mask: int32 [64], P('parts'), parts along dimension 0, may hold values from 0 to 1, as said below
- w_tri_in: bfloat16 [128, 512], replicated, may hold values from -0.5 to 0.5
- w_tri_gate: bfloat16 [128, 128], replicated, may hold values from -0.5 to 0.5
- w_tri_out: bfloat16 [128, 128], replicated, may hold values from -0.5 to 0.5
- w_qkv: bfloat16 [128, 384], replicated, may hold values from -0.5 to 0.5
- w_att_bias: bfloat16 [128, 4], replicated, may hold values from -80 to 80
- w_att_gate: bfloat16 [128, 128], replicated, may hold values from -0.5 to 0.5
- w_att_out: bfloat16 [128, 128], replicated, may hold values from -0.5 to 0.5
Outputs:
- updated: bfloat16 [64, 32, 128], P(('parts', 'rows')), parts along dimension 0
There are 2 independent parts, one for each index of `parts`. A program takes and returns all parts, laid end to end along the dimension named above; an argument that names none is the same for every part. Nothing has to cross between parts.
Inputs may be any that keep to these rules, and one draw needn't show every extreme that they name: `mask`: 0 on every residue from some L on, with 16 <= L <= 31; before L each residue may be 1 or 0 (unresolved); residue 0 is always 1.
All inputs are finite; a program needn't handle non-finite values.
Results may differ from a plain program's by a relative error of at most 0.012.
Values may be sent and summed in bfloat16 or wider, within the bound.
A program may use at most 64 MiB of HBM per device.

v0:
```python
import jax
import jax.numpy as jnp
from jax import lax
from jax.sharding import PartitionSpec as P

HEADS = 4
HEAD_DIM = 32
EPSILON = 1e-05
MASK_PENALTY = 1000000000.0


def normalize(values, along_axis):
    values = values.astype(jnp.float32)
    center = jnp.mean(values, axis=along_axis, keepdims=True)
    shifted = values - center
    spread = jnp.mean(shifted * shifted, axis=along_axis, keepdims=True)
    return shifted * lax.rsqrt(spread + EPSILON)


def attend(queries, key_rows, values, score_bias, key_penalty, score_scale):
    column_count = queries.shape[1]
    heads_here = queries.shape[2]
    block_size = max(1, 4 // heads_here)

    def reorder(tensor):
        return tensor.reshape(
            tensor.shape[0], column_count // block_size, block_size, heads_here, -1
        ).transpose(1, 0, 2, 3, 4)

    def one_block(inputs):
        query_part, key_part, value_part = inputs
        scores = (
            jnp.einsum("kbhd,ibhd->bhki", key_part, query_part, preferred_element_type=jnp.float32)
            * score_scale
        )
        scores = scores + score_bias[None] + key_penalty[None, None, :, None]
        row_peak = jnp.max(scores, axis=2, keepdims=True)
        weights = jnp.exp(scores - row_peak)
        weights = (weights / jnp.sum(weights, axis=2, keepdims=True)).astype(jnp.bfloat16)
        result = jnp.einsum(
            "bhki,kbhd->ibhd", weights, value_part, preferred_element_type=jnp.float32
        )
        return result.astype(jnp.bfloat16)

    outputs = lax.map(one_block, (reorder(queries), reorder(key_rows), reorder(values)))
    return outputs.transpose(1, 0, 2, 3, 4).reshape(queries.shape)


def local(pair, mask, w_tri_in, w_tri_gate, w_tri_out, w_qkv, w_att_bias, w_att_gate, w_att_out):
    row_count = pair.shape[0]
    residues = pair.shape[1]
    devices = lax.axis_size("rows")
    first_row = lax.axis_index("rows") * row_count
    key_mask = mask.astype(jnp.float32)
    row_mask = lax.dynamic_slice_in_dim(key_mask, first_row, row_count, 0)
    key_penalty = (key_mask - 1.0) * MASK_PENALTY
    normed = normalize(pair, 2).astype(jnp.bfloat16)
    projected = jnp.einsum("rkc,cf->frk", normed, w_tri_in, preferred_element_type=jnp.float32)
    hidden = w_tri_out.shape[0]
    pair_mask = row_mask[:, None] * key_mask[None, :]
    left_side = (
        jax.nn.sigmoid(projected[:hidden]) * projected[hidden : 2 * hidden] * pair_mask
    ).astype(jnp.bfloat16)
    right_side = (
        jax.nn.sigmoid(projected[2 * hidden : 3 * hidden]) * projected[3 * hidden :] * pair_mask
    ).astype(jnp.bfloat16)
    left_cols, right_cols = (
        lax.all_to_all(left_side, "rows", split_axis=0, concat_axis=1, tiled=True),
        lax.all_to_all(right_side, "rows", split_axis=0, concat_axis=1, tiled=True),
    )
    product = jnp.einsum(
        "cik,cjk->cij", left_cols, right_cols, preferred_element_type=jnp.float32
    ).astype(jnp.bfloat16)
    triangle_rows = lax.all_to_all(product, "rows", split_axis=1, concat_axis=0, tiled=True)
    triangle_normed = normalize(triangle_rows, 0).astype(jnp.bfloat16)
    triangle_gate = jax.nn.sigmoid(
        jnp.einsum("rjc,cd->rjd", normed, w_tri_gate, preferred_element_type=jnp.float32)
    )
    triangle_update = jnp.einsum(
        "crj,cd->rjd", triangle_normed, w_tri_out, preferred_element_type=jnp.float32
    )
    middle = lax.optimization_barrier(
        (pair.astype(jnp.float32) + triangle_gate * triangle_update).astype(jnp.bfloat16)
    )
    attention_input = normalize(middle, 2).astype(jnp.bfloat16)
    bias_rows = jnp.einsum(
        "kic,ch->hki", attention_input, w_att_bias, preferred_element_type=jnp.float32
    )
    score_scale = HEAD_DIM ** (-0.5)
    groups = devices // HEADS
    group_width = residues // groups
    projections = jnp.einsum(
        "rgwc,cthd->hgrtwd",
        attention_input.reshape(row_count, groups, group_width, -1),
        w_qkv.reshape(-1, 3, HEADS, HEAD_DIM),
        preferred_element_type=jnp.float32,
    ).astype(jnp.bfloat16)
    outgoing = projections.reshape(devices, row_count, 3, group_width * HEAD_DIM)
    received = lax.all_to_all(outgoing, "rows", split_axis=0, concat_axis=1, tiled=True)
    bias_copies = jnp.repeat(bias_rows, groups, axis=0)
    head_bias = lax.all_to_all(bias_copies, "rows", split_axis=0, concat_axis=1, tiled=True)
    pieces = received.reshape(residues, 3, group_width, 1, HEAD_DIM)
    attended = attend(pieces[:, 0], pieces[:, 1], pieces[:, 2], head_bias, key_penalty, score_scale)
    returned = lax.all_to_all(
        attended.reshape(residues, group_width, HEAD_DIM),
        "rows",
        split_axis=0,
        concat_axis=1,
        tiled=True,
    )
    attention_rows = (
        returned.reshape(row_count, HEADS, groups, group_width, HEAD_DIM)
        .transpose(0, 2, 3, 1, 4)
        .reshape(row_count, residues, HEADS * HEAD_DIM)
    )
    attention_gate = jax.nn.sigmoid(
        jnp.einsum("rjc,cf->rjf", attention_input, w_att_gate, preferred_element_type=jnp.float32)
    )
    gated_output = (attention_gate * attention_rows.astype(jnp.float32)).astype(jnp.bfloat16)
    result = middle.astype(jnp.float32) + jnp.einsum(
        "rjf,fc->rjc", gated_output, w_att_out, preferred_element_type=jnp.float32
    )
    return result.astype(jnp.bfloat16)


def solution(mesh):
    placed = (P(("parts", "rows"), None, None), P("parts"), P(), P(), P(), P(), P(), P(), P())
    return jax.shard_map(
        local,
        mesh=mesh,
        in_specs=placed,
        out_specs=P(("parts", "rows"), None, None),
        check_vma=False,
    )
```

profile of v0, /device:TPU:0, one launch (start us, length us, event | category | flops | bytes accessed | tf_op | source)
XLA Modules:
  0.0 73.1 jit_solution(14103554241699838095)
XLA Ops:
  0.0 0.7 convert_element_type.92
  1.0 0.2 fusion.50
  1.1 0.2 convolution_bitcast_fusion
  1.4 0.1 copy.52
  1.6 0.7 reshape.158
  2.3 7.4 %all-to-all-start = ((bf16[16,2,256]{2,1,0:T(2,128)(2,1)}), bf16[16,2,256]{2,1,0:T(2,128)(2,1)S(1)}, u32[]{:S(2)}, u32[]{:S(2)}) async-start(bf16[16,2,256]{2,1,0:T(2,128)(2,1)} %reshape.158), calls=%async_computation | async-start | bytes 32768 | tf_op jit(solution)/shard_map/all_to_all | solution.py:68
  9.7 0.1 copy.55
  9.8 0.7 reshape.160
  10.5 5.7 %all-to-all-done = bf16[16,2,256]{2,1,0:T(2,128)(2,1)S(1)} async-done(((bf16[16,2,256]{2,1,0:T(2,128)(2,1)}), bf16[16,2,256]{2,1,0:T(2,128)(2,1)S(1)}, u32[]{:S(2)}, u32[]{:S(2)}) %all-to-all-start) | async-done | bytes 16416 | tf_op jit(solution)/shard_map/all_to_all | solution.py:68
  16.2 3.5 %all-to-all-start.1 = ((bf16[16,2,256]{2,1,0:T(2,128)(2,1)}), bf16[16,2,256]{2,1,0:T(2,128)(2,1)S(1)}, u32[]{:S(2)}, u32[]{:S(2)}) async-start(bf16[16,2,256]{2,1,0:T(2,128)(2,1)} %reshape.160), calls=%async_computation.1 | async-start | bytes 32768 | tf_op jit(solution)/shard_map/all_to_all | solution.py:69
  19.7 0.2 fusion.32
  19.9 0.1 reshape.159
  20.1 6.0 %all-to-all-done.1 = bf16[16,2,256]{2,1,0:T(2,128)(2,1)S(1)} async-done(((bf16[16,2,256]{2,1,0:T(2,128)(2,1)}), bf16[16,2,256]{2,1,0:T(2,128)(2,1)S(1)}, u32[]{:S(2)}, u32[]{:S(2)}) %all-to-all-start.1) | async-done | bytes 16416 | tf_op jit(solution)/shard_map/all_to_all | solution.py:69
  26.2 0.1 reshape.161
  26.4 0.2 convolution_convert_fusion.2
  26.6 0.7 reshape.162
  27.3 3.6 %all-to-all-start.2 = ((bf16[16,2,256]{2,1,0:T(2,128)(2,1)}), bf16[16,2,256]{2,1,0:T(2,128)(2,1)S(1)}, u32[]{:S(2)}, u32[]{:S(2)}) async-start(bf16[16,2,256]{2,1,0:T(2,128)(2,1)} %reshape.162), calls=%async_computation.2 | async-start | bytes 32768 | tf_op jit(solution)/shard_map/all_to_all | solution.py:74
  31.0 0.1 copy.61
  31.1 6.3 %all-to-all-done.2 = bf16[16,2,256]{2,1,0:T(2,128)(2,1)S(1)} async-done(((bf16[16,2,256]{2,1,0:T(2,128)(2,1)}), bf16[16,2,256]{2,1,0:T(2,128)(2,1)S(1)}, u32[]{:S(2)}, u32[]{:S(2)}) %all-to-all-start.2) | async-done | bytes 16416 | tf_op jit(solution)/shard_map/all_to_all | solution.py:74
  37.4 0.1 reshape.163
  37.6 0.7 copy-done.4
  38.3 0.2 fusion.33
  38.5 0.1 convert_reduce_fusion
  38.6 0.2 fusion.48
  38.8 0.3 fusion.24
  39.1 0.8 %reshape.157 = bf16[16,2,3,256]{3,1,2,0:T(2,128)(2,1)} reshape(bf16[4,4,2,3,8,32]{5,4,2,3,1,0:T(8,128)(2,1)S(1)} %copy.75) | data formatting | bytes 98304 | tf_op jit(solution)/shard_map/reshape | solution.py:98
  39.9 3.6 %all-to-all-start.3 = ((bf16[16,2,3,256]{3,1,2,0:T(2,128)(2,1)}), bf16[16,2,3,256]{3,1,2,0:T(2,128)(2,1)S(1)}, u32[]{:S(2)}, u32[]{:S(2)}) async-start(bf16[16,2,3,256]{3,1,2,0:T(2,128)(2,1)} %reshape.157), calls=%async_computation.3 | async-start | bytes 98304 | tf_op jit(solution)/shard_map/all_to_all | solution.py:99
  43.6 0.2 convolution_bitcast_fusion.1
  43.8 6.5 %all-to-all-done.3 = bf16[16,2,3,256]{3,1,2,0:T(2,128)(2,1)S(1)} async-done(((bf16[16,2,3,256]{3,1,2,0:T(2,128)(2,1)}), bf16[16,2,3,256]{3,1,2,0:T(2,128)(2,1)S(1)}, u32[]{:S(2)}, u32[]{:S(2)}) %all-to-all-start.3) | async-done | bytes 49184 | tf_op jit(solution)/shard_map/all_to_all | solution.py:99
  50.3 0.6 broadcast_in_dim.8
  50.9 3.5 %all-to-all-start.4 = ((f32[16,2,32]{2,1,0:T(2,128)}), f32[16,2,32]{2,1,0:T(2,128)S(1)}, u32[]{:S(2)}, u32[]{:S(2)}) async-start(f32[16,2,32]{2,1,0:T(2,128)} %bitcast.36), calls=%async_computation.4 | async-start | bytes 32768 | tf_op jit(solution)/shard_map/all_to_all | solution.py:101
  54.4 0.2 reshape.141
  54.6 0.1 copy.65
  54.8 6.1 %all-to-all-done.4 = f32[16,2,32]{2,1,0:T(2,128)S(1)} async-done(((f32[16,2,32]{2,1,0:T(2,128)}), f32[16,2,32]{2,1,0:T(2,128)S(1)}, u32[]{:S(2)}, u32[]{:S(2)}) %all-to-all-start.4) | async-done | bytes 4128 | tf_op jit(solution)/shard_map/all_to_all | solution.py:101
  60.9 1.0 %while.10 = (s32[]{:T(128)}, bf16[2,32,4,1,32]{1,4,2,3,0:T(8,128)(2,1)S(1)}, bf16[2,32,4,1,32]{1,4,2,3,0:T(8,128)(2,1)S(1)}, bf16[2,32,4,1,32]{4,1,2,3,0:T(8,128...) while((s32[]{:T(128)}, ...), condition=%wide.region_9.10_spmd, body=%wide.region_6.9_spmd.sunk | while | flops 835776 | bytes 383573 | solution.py:45
  60.9 0.1 fusion.111
  61.0 0.2 fusion.110
  61.2 0.2 fusion.112
  61.4 0.1 fusion.111
  61.5 0.2 fusion.110
  61.7 0.2 fusion.112
  61.8 0.1 copy.69
  62.0 0.1 reshape.164
  62.1 9.1 %all_to_all.78 = bf16[16,2,256]{2,1,0:T(2,128)(2,1)S(1)} all-to-all(bf16[16,2,256]{2,1,0:T(2,128)(2,1)S(1)} %reshape.164), channel_id=1, replica_groups=mesh['parts'=2,'rows'=16] {'rows'}, dimensions={0} | all-to-all | bytes 32768 | tf_op jit(solution)/shard_map/all_to_all | solution.py:104
  71.1 0.1 reshape.165
  71.4 0.1 reshape.144
  71.5 0.6 copy-done.5
  72.1 0.9 %fusion.35 = bf16[2,32,128]{2,1,0:T(8,128)(2,1)} fusion(f32[2,32,128]{2,1,0:T(8,128)S(1)} %reshape.144, bf16[2,32,128]{2,1,0:T(8,128)(2,1)S(1)} %fusion.33, bf16[128,128]{1,0:T(8,128)(2,1)S(1)} %copy-done.5, bf16[128,128]{1,0:T(8,128)(2,1)S(1)} %copy-done.6, f32[2,32]{1,0:T(2,128)S(1)} %add_rsqrt_fusion, f32[2,32]{1,0:T(2,128)S(1)} %broadcast_multiply_fusion.1), kind=kOutput, calls=%fused_computation.40 | convolution fusion | flops 4292608 | bytes 131584 | tf_op jit(solution)/shard_map/rjf,fc->rjc/dot_general | solution.py:120
  (43 shorter events, 0.9 us)
Async XLA Ops:
  0.0 1.1 %copy-start = (bf16[128,512]{1,0:T(8,128)(2,1)S(1)}, bf16[128,512]{1,0:T(8,128)(2,1)}, u32[]{:S(2)}) copy-start(bf16[128,512]{1,0:T(8,128)(2,1)} %param.13) | copy-start | bytes 393220
  0.0 0.9 %copy-start.1 = (bf16[2,32,128]{2,1,0:T(8,128)(2,1)S(1)}, bf16[2,32,128]{2,1,0:T(8,128)(2,1)}, u32[]{:S(2)}) copy-start(bf16[2,32,128]{2,1,0:T(8,128)(2,1)} %param.11) | copy-start | bytes 49156
  2.3 13.9 %all-to-all-start = ((bf16[16,2,256]{2,1,0:T(2,128)(2,1)}), bf16[16,2,256]{2,1,0:T(2,128)(2,1)S(1)}, u32[]{:S(2)}, u32[]{:S(2)}) async-start(bf16[16,2,256]{2,1,0:T(2,128)(2,1)} %reshape.158), calls=%async_computation | async-start | bytes 32768 | tf_op jit(solution)/shard_map/all_to_all | solution.py:68
  10.5 9.2 %copy-start.3 = (bf16[128,128]{1,0:T(8,128)(2,1)S(1)}, bf16[128,128]{1,0:T(8,128)(2,1)}, u32[]{:S(2)}) copy-start(bf16[128,128]{1,0:T(8,128)(2,1)} %param.14) | copy-start | bytes 98308
  16.2 10.0 %all-to-all-start.1 = ((bf16[16,2,256]{2,1,0:T(2,128)(2,1)}), bf16[16,2,256]{2,1,0:T(2,128)(2,1)S(1)}, u32[]{:S(2)}, u32[]{:S(2)}) async-start(bf16[16,2,256]{2,1,0:T(2,128)(2,1)} %reshape.160), calls=%async_computation.1 | async-start | bytes 32768 | tf_op jit(solution)/shard_map/all_to_all | solution.py:69
  26.5 4.4 %copy-start.2 = (bf16[128,384]{1,0:T(8,128)(2,1)S(1)}, bf16[128,384]{1,0:T(8,128)(2,1)}, u32[]{:S(2)}) copy-start(bf16[128,384]{1,0:T(8,128)(2,1)} %param.16) | copy-start | bytes 294916
  27.3 3.6 %copy-start.8 = (s32[32]{0:T(128)S(1)}, s32[32]{0:T(128)}, u32[]{:S(2)}) copy-start(s32[32]{0:T(128)} %param.12) | copy-start | bytes 388
  27.3 10.1 %all-to-all-start.2 = ((bf16[16,2,256]{2,1,0:T(2,128)(2,1)}), bf16[16,2,256]{2,1,0:T(2,128)(2,1)S(1)}, u32[]{:S(2)}, u32[]{:S(2)}) async-start(bf16[16,2,256]{2,1,0:T(2,128)(2,1)} %reshape.162), calls=%async_computation.2 | async-start | bytes 32768 | tf_op jit(solution)/shard_map/all_to_all | solution.py:74
  37.6 0.8 %copy-start.4 = (bf16[128,128]{1,0:T(8,128)(2,1)S(1)}, bf16[128,128]{1,0:T(8,128)(2,1)}, u32[]{:S(2)}) copy-start(bf16[128,128]{1,0:T(8,128)(2,1)} %param.15) | copy-start | bytes 98308
  39.9 3.6 %copy-start.7 = (bf16[128,4]{0,1:T(4,128)(2,1)S(1)}, bf16[128,4]{0,1:T(4,128)(2,1)}, u32[]{:S(2)}) copy-start(bf16[128,4]{0,1:T(4,128)(2,1)} %param.17) | copy-start | bytes 3076
  39.9 10.4 %all-to-all-start.3 = ((bf16[16,2,3,256]{3,1,2,0:T(2,128)(2,1)}), bf16[16,2,3,256]{3,1,2,0:T(2,128)(2,1)S(1)}, u32[]{:S(2)}, u32[]{:S(2)}) async-start(bf16[16,2,3,256]{3,1,2,0:T(2,128)(2,1)} %reshape.157), calls=%async_computation.3 | async-start | bytes 98304 | tf_op jit(solution)/shard_map/all_to_all | solution.py:99
  50.9 10.0 %all-to-all-start.4 = ((f32[16,2,32]{2,1,0:T(2,128)}), f32[16,2,32]{2,1,0:T(2,128)S(1)}, u32[]{:S(2)}, u32[]{:S(2)}) async-start(f32[16,2,32]{2,1,0:T(2,128)} %bitcast.36), calls=%async_computation.4 | async-start | bytes 32768 | tf_op jit(solution)/shard_map/all_to_all | solution.py:101
  71.4 0.8 %copy-start.5 = (bf16[128,128]{1,0:T(8,128)(2,1)S(1)}, bf16[128,128]{1,0:T(8,128)(2,1)}, u32[]{:S(2)}) copy-start(bf16[128,128]{1,0:T(8,128)(2,1)} %param.19) | copy-start | bytes 98308
  71.4 0.8 %copy-start.6 = (bf16[128,128]{1,0:T(8,128)(2,1)S(1)}, bf16[128,128]{1,0:T(8,128)(2,1)}, u32[]{:S(2)}) copy-start(bf16[128,128]{1,0:T(8,128)(2,1)} %param.18) | copy-start | bytes 98308
where the time goes:
time: 73.7 us; the launch traced here: 73.1 us
  waiting for transfers between devices  30.6 us (42%)
  starting transfers between devices  21.7 us (29%)
  blocking collectives  9.07 us (12%)
  local copies, waits for them, and re-layouts  6.74 us (9%)
  matrix products  3.16 us (4%)
  other arithmetic  1.51 us (2%)
    all_to_all x1, blocking collectives, local(): lax.all_to_all(attended.reshape(residues, group_width, HEAD_DIM), 'rows',...  9.07 us
    all_to_all x1, starting transfers between devices, local(): lax.all_to_all(left_side, 'rows', split_axis=0, concat_axis=1, tiled=True)  7.41 us
    all_to_all x1, waiting for transfers between devices, local(): lax.all_to_all(outgoing, 'rows', split_axis=0, concat_axis=1, tiled=True)  6.51 us
    all_to_all x1, waiting for transfers between devices, local(): lax.all_to_all(product, 'rows', split_axis=1, concat_axis=0, tiled=True)  6.3 us
    all_to_all x1, waiting for transfers between devices, local(): lax.all_to_all(bias_copies, 'rows', split_axis=0, concat_axis=1, tiled=True)  6.08 us
    all_to_all x1, waiting for transfers between devices, local(): lax.all_to_all(right_side, 'rows', split_axis=0, concat_axis=1, tiled=True)  6.03 us
    all_to_all x1, waiting for transfers between devices, local(): lax.all_to_all(left_side, 'rows', split_axis=0, concat_axis=1, tiled=True)  5.67 us
    unnamed x27, local copies, waits for them, and re-layouts  4.13 us
  transfers between devices with their start and end apart: 5, of which 5 were waited for; matrix products, arithmetic and copies ran while one was open for 3% of the time, Pallas kernels for 0%

commit v1 on v0

--- a/solution.py
+++ b/solution.py
@@ -7,6 +7,27 @@
 HEAD_DIM = 32
 EPSILON = 1e-05
 MASK_PENALTY = 1000000000.0
+
+
+def attach_strips_all(array_here, axis_tag, row_dim, array_dim):
+    reply = lax.axis_index(axis_tag)
+    s_next = lax.axis_size(axis_tag)
+    local_out, formed = (s_next, reply)
+    frame_out = list(array_here.shape)
+    spare = array_here.shape[row_dim] // local_out
+    frame_out[row_dim] = spare
+    local_now = frame_out[array_dim]
+    frame_out[array_dim] = local_now * local_out
+    heard = jnp.zeros(frame_out, array_here.dtype)
+    for pp in range(local_out):
+        h_now = lax.dynamic_slice_in_dim(array_here, (formed ^ pp) * spare, spare, axis=row_dim)
+        if pp:
+            v1 = tuple(((j0, j0 ^ pp) for j0 in range(local_out)))
+            h_now = lax.ppermute(h_now, axis_tag, v1)
+        heard = lax.dynamic_update_slice_in_dim(
+            heard, h_now, (formed ^ pp) * local_now, axis=array_dim
+        )
+    return heard
 
 
 def normalize(values, along_axis):
@@ -101,13 +122,7 @@
     head_bias = lax.all_to_all(bias_copies, "rows", split_axis=0, concat_axis=1, tiled=True)
     pieces = received.reshape(residues, 3, group_width, 1, HEAD_DIM)
     attended = attend(pieces[:, 0], pieces[:, 1], pieces[:, 2], head_bias, key_penalty, score_scale)
-    returned = lax.all_to_all(
-        attended.reshape(residues, group_width, HEAD_DIM),
-        "rows",
-        split_axis=0,
-        concat_axis=1,
-        tiled=True,
-    )
+    returned = attach_strips_all(attended.reshape(residues, group_width, HEAD_DIM), "rows", 0, 1)
     attention_rows = (
         returned.reshape(row_count, HEADS, groups, group_width, HEAD_DIM)
         .transpose(0, 2, 3, 1, 4)

time: 73.7 us -> 86.9 us (1.18)
  starting transfers between devices: 21.7 us -> 42 us
  blocking collectives: 9.07 us -> 0 us
    ppermute x0 -> x15, starting transfers between devices: none -> 20.4 us  [attach_strips_all(): h_now = lax.ppermute(h_now, axis_tag, v1)]
    all_to_all x1 -> x0, blocking collectives: 9.07 us -> none  [local(): lax.all_to_all(attended.reshape(residues, group_width, HEAD_DIM), 'rows',...]
    ppermute x0 -> x15, waiting for transfers between devices: none -> 1.85 us  [attach_strips_all(): h_now = lax.ppermute(h_now, axis_tag, v1)]
    all_to_all x1, waiting for transfers between devices: 6.3 us -> 5.3 us  [local(): lax.all_to_all(product, 'rows', split_axis=1, concat_axis=0, tiled=True)]
    unnamed x27 -> x25, local copies, waits for them, and re-layouts: 4.13 us -> 4.69 us
  transfers between devices with their start and end apart: 5 -> 20, of which waited for: 5 -> 6; matrix products, arithmetic and copies ran while one was open for 3% -> 2% of each run, Pallas kernels for 0% -> 0%
where the time goes in v1:
time: 86.9 us; the launch traced here: 86.3 us
  starting transfers between devices  42 us (48%)
  waiting for transfers between devices  31.4 us (36%)
  local copies, waits for them, and re-layouts  7.53 us (9%)
  matrix products  3.15 us (4%)
  other arithmetic  1.51 us (2%)
    ppermute x15, starting transfers between devices, attach_strips_all(): h_now = lax.ppermute(h_now, axis_tag, v1)  20.4 us
    all_to_all x1, starting transfers between devices, local(): lax.all_to_all(left_side, 'rows', split_axis=0, concat_axis=1, tiled=True)  7.41 us
    all_to_all x1, waiting for transfers between devices, local(): lax.all_to_all(outgoing, 'rows', split_axis=0, concat_axis=1, tiled=True)  6.51 us
    all_to_all x1, waiting for transfers between devices, local(): lax.all_to_all(bias_copies, 'rows', split_axis=0, concat_axis=1, tiled=True)  6.08 us
    all_to_all x1, waiting for transfers between devices, local(): lax.all_to_all(right_side, 'rows', split_axis=0, concat_axis=1, tiled=True)  6.03 us
    all_to_all x1, waiting for transfers between devices, local(): lax.all_to_all(left_side, 'rows', split_axis=0, concat_axis=1, tiled=True)  5.67 us
    all_to_all x1, waiting for transfers between devices, local(): lax.all_to_all(product, 'rows', split_axis=1, concat_axis=0, tiled=True)  5.3 us
    unnamed x25, local copies, waits for them, and re-layouts  4.69 us
  transfers between devices with their start and end apart: 20, of which 6 were waited for; matrix products, arithmetic and copies ran while one was open for 2% of the time, Pallas kernels for 0%

profile of v1, /device:TPU:0, one launch (start us, length us, event | category | flops | bytes accessed | tf_op | source)
XLA Modules:
  0.0 86.3 jit_solution(13476869169215087440)
XLA Ops:
  0.0 0.7 convert_element_type.89
  1.0 0.2 fusion.50
  1.1 0.2 convolution_bitcast_fusion
  1.6 0.7 reshape.156
  2.3 7.4 %all-to-all-start = ((bf16[16,2,256]{2,1,0:T(2,128)(2,1)}), bf16[16,2,256]{2,1,0:T(2,128)(2,1)S(1)}, u32[]{:S(2)}, u32[]{:S(2)}) async-start(bf16[16,2,256]{2,1,0:T(2,128)(2,1)} %reshape.156), calls=%async_computation | async-start | bytes 32768 | tf_op jit(solution)/shard_map/all_to_all | solution.py:89
  9.8 0.7 reshape.158
  10.5 5.7 %all-to-all-done = bf16[16,2,256]{2,1,0:T(2,128)(2,1)S(1)} async-done(((bf16[16,2,256]{2,1,0:T(2,128)(2,1)}), bf16[16,2,256]{2,1,0:T(2,128)(2,1)S(1)}, u32[]{:S(2)}, u32[]{:S(2)}) %all-to-all-start) | async-done | bytes 16416 | tf_op jit(solution)/shard_map/all_to_all | solution.py:89
  16.2 3.4 %all-to-all-start.1 = ((bf16[16,2,256]{2,1,0:T(2,128)(2,1)}), bf16[16,2,256]{2,1,0:T(2,128)(2,1)S(1)}, u32[]{:S(2)}, u32[]{:S(2)}) async-start(bf16[16,2,256]{2,1,0:T(2,128)(2,1)} %reshape.158), calls=%async_computation.1 | async-start | bytes 32768 | tf_op jit(solution)/shard_map/all_to_all | solution.py:90
  19.7 0.2 fusion.32
  20.1 6.0 %all-to-all-done.1 = bf16[16,2,256]{2,1,0:T(2,128)(2,1)S(1)} async-done(((bf16[16,2,256]{2,1,0:T(2,128)(2,1)}), bf16[16,2,256]{2,1,0:T(2,128)(2,1)S(1)}, u32[]{:S(2)}, u32[]{:S(2)}) %all-to-all-start.1) | async-done | bytes 16416 | tf_op jit(solution)/shard_map/all_to_all | solution.py:90
  26.5 0.7 reshape.160
  27.2 3.6 %all-to-all-start.2 = ((bf16[16,2,256]{2,1,0:T(2,128)(2,1)}), bf16[16,2,256]{2,1,0:T(2,128)(2,1)S(1)}, u32[]{:S(2)}, u32[]{:S(2)}) async-start(bf16[16,2,256]{2,1,0:T(2,128)(2,1)} %reshape.160), calls=%async_computation.2 | async-start | bytes 32768 | tf_op jit(solution)/shard_map/all_to_all | solution.py:95
  31.0 0.8 copy-done.2
  32.0 5.3 %all-to-all-done.2 = bf16[16,2,256]{2,1,0:T(2,128)(2,1)S(1)} async-done(((bf16[16,2,256]{2,1,0:T(2,128)(2,1)}), bf16[16,2,256]{2,1,0:T(2,128)(2,1)S(1)}, u32[]{:S(2)}, u32[]{:S(2)}) %all-to-all-start.2) | async-done | bytes 16416 | tf_op jit(solution)/shard_map/all_to_all | solution.py:95
  37.5 0.7 copy-done.4
  38.2 0.2 fusion.33
  38.5 0.2 fusion.48
  38.7 0.3 fusion.24
  39.1 0.8 reshape.155
  39.8 3.6 %all-to-all-start.3 = ((bf16[16,2,3,256]{3,1,2,0:T(2,128)(2,1)}), bf16[16,2,3,256]{3,1,2,0:T(2,128)(2,1)S(1)}, u32[]{:S(2)}, u32[]{:S(2)}) async-start(bf16[16,2,3,256]{3,1,2,0:T(2,128)(2,1)} %reshape.155), calls=%async_computation.3 | async-start | bytes 98304 | tf_op jit(solution)/shard_map/all_to_all | solution.py:120
  43.5 0.2 convolution_bitcast_fusion.1
  43.7 6.5 %all-to-all-done.3 = bf16[16,2,3,256]{3,1,2,0:T(2,128)(2,1)S(1)} async-done(((bf16[16,2,3,256]{3,1,2,0:T(2,128)(2,1)}), bf16[16,2,3,256]{3,1,2,0:T(2,128)(2,1)S(1)}, u32[]{:S(2)}, u32[]{:S(2)}) %all-to-all-start.3) | async-done | bytes 49184 | tf_op jit(solution)/shard_map/all_to_all | solution.py:120
  50.2 0.6 broadcast_in_dim.11
  50.8 3.5 %all-to-all-start.4 = ((f32[16,2,32]{2,1,0:T(2,128)}), f32[16,2,32]{2,1,0:T(2,128)S(1)}, u32[]{:S(2)}, u32[]{:S(2)}) async-start(f32[16,2,32]{2,1,0:T(2,128)} %bitcast.36), calls=%async_computation.4 | async-start | bytes 32768 | tf_op jit(solution)/shard_map/all_to_all | solution.py:122
  54.3 0.2 reshape.140
  54.7 6.1 %all-to-all-done.4 = f32[16,2,32]{2,1,0:T(2,128)S(1)} async-done(((f32[16,2,32]{2,1,0:T(2,128)}), f32[16,2,32]{2,1,0:T(2,128)S(1)}, u32[]{:S(2)}, u32[]{:S(2)}) %all-to-all-start.4) | async-done | bytes 4128 | tf_op jit(solution)/shard_map/all_to_all | solution.py:122
  60.8 1.0 %while.10 = (s32[]{:T(128)}, bf16[2,32,4,1,32]{1,4,2,3,0:T(8,128)(2,1)S(1)}, bf16[2,32,4,1,32]{1,4,2,3,0:T(8,128)(2,1)S(1)}, bf16[2,32,4,1,32]{4,1,2,3,0:T(8,128...) while((s32[]{:T(128)}, ...), condition=%wide.region_9.10_spmd, body=%wide.region_6.9_spmd.sunk | while | flops 835776 | bytes 383573 | solution.py:66
  60.9 0.2 fusion.110
  61.1 0.2 fusion.112
  61.4 0.2 fusion.110
  61.6 0.2 fusion.112
  62.1 0.5 collective-permute-start.1
  62.7 1.3 %collective-permute-start.2 = (bf16[2,8,32]{2,1,0:T(8,128)(2,1)S(1)}, bf16[2,8,32]{2,1,0:T(8,128)(2,1)S(1)}, u32[]{:S(2)}, u32[]{:S(2)}) collective-permute-start(bf16[2,8,32]{2,1,0:T(8,128)(2,1)S(1)} %get-tuple-element.74), channel_id=1, source_target_pairs={{0,3},{1,2},{2,1},{3,0},{4,7},{5,6},{6,5},{7,4},{8,11},{9,10},{10,... | collective-permute-start | bytes 3080 | tf_op jit(solution)/shard_map/ppermute | solution.py:26
  63.9 0.5 collective-permute-start.3
  64.4 1.3 %collective-permute-start.4 = (bf16[2,8,32]{2,1,0:T(8,128)(2,1)S(1)}, bf16[2,8,32]{2,1,0:T(8,128)(2,1)S(1)}, u32[]{:S(2)}, u32[]{:S(2)}) collective-permute-start(bf16[2,8,32]{2,1,0:T(8,128)(2,1)S(1)} %get-tuple-element.72), channel_id=1, source_target_pairs={{0,5},{1,4},{2,7},{3,6},{4,1},{5,0},{6,3},{7,2},{8,13},{9,12},{10,... | collective-permute-start | bytes 3080 | tf_op jit(solution)/shard_map/ppermute | solution.py:26
  65.7 0.5 collective-permute-start.5
  66.2 2.1 %collective-permute-start.6 = (bf16[2,8,32]{2,1,0:T(8,128)(2,1)S(1)}, bf16[2,8,32]{2,1,0:T(8,128)(2,1)S(1)}, u32[]{:S(2)}, u32[]{:S(2)}) collective-permute-start(bf16[2,8,32]{2,1,0:T(8,128)(2,1)S(1)} %get-tuple-element.70), channel_id=1, source_target_pairs={{0,7},{1,6},{2,5},{3,4},{4,3},{5,2},{6,1},{7,0},{8,15},{9,14},{10,... | collective-permute-start | bytes 3080 | tf_op jit(solution)/shard_map/ppermute | solution.py:26
  68.3 0.5 collective-permute-start.7
  68.8 2.2 %collective-permute-start.8 = (bf16[2,8,32]{2,1,0:T(8,128)(2,1)S(1)}, bf16[2,8,32]{2,1,0:T(8,128)(2,1)S(1)}, u32[]{:S(2)}, u32[]{:S(2)}) collective-permute-start(bf16[2,8,32]{2,1,0:T(8,128)(2,1)S(1)} %get-tuple-element.68), channel_id=1, source_target_pairs={{0,9},{1,8},{2,11},{3,10},{4,13},{5,12},{6,15},{7,14},{8,1},{9,0},... | collective-permute-start | bytes 3080 | tf_op jit(solution)/shard_map/ppermute | solution.py:26
  71.0 0.5 collective-permute-start.9
  71.5 3.0 %collective-permute-start.10 = (bf16[2,8,32]{2,1,0:T(8,128)(2,1)S(1)}, bf16[2,8,32]{2,1,0:T(8,128)(2,1)S(1)}, u32[]{:S(2)}, u32[]{:S(2)}) collective-permute-start(bf16[2,8,32]{2,1,0:T(8,128)(2,1)S(1)} %get-tuple-element.66), channel_id=1, source_target_pairs={{0,11},{1,10},{2,9},{3,8},{4,15},{5,14},{6,13},{7,12},{8,3},{9,2},... | collective-permute-start | bytes 3080 | tf_op jit(solution)/shard_map/ppermute | solution.py:26
  74.6 0.5 collective-permute-start.11
  75.1 3.1 %collective-permute-start.12 = (bf16[2,8,32]{2,1,0:T(8,128)(2,1)S(1)}, bf16[2,8,32]{2,1,0:T(8,128)(2,1)S(1)}, u32[]{:S(2)}, u32[]{:S(2)}) collective-permute-start(bf16[2,8,32]{2,1,0:T(8,128)(2,1)S(1)} %get-tuple-element.64), channel_id=1, source_target_pairs={{0,13},{1,12},{2,15},{3,14},{4,9},{5,8},{6,11},{7,10},{8,5},{9,4},... | collective-permute-start | bytes 3080 | tf_op jit(solution)/shard_map/ppermute | solution.py:26
  78.2 0.5 collective-permute-start.13
  78.7 3.9 %collective-permute-start.14 = (bf16[2,8,32]{2,1,0:T(8,128)(2,1)S(1)}, bf16[2,8,32]{2,1,0:T(8,128)(2,1)S(1)}, u32[]{:S(2)}, u32[]{:S(2)}) collective-permute-start(bf16[2,8,32]{2,1,0:T(8,128)(2,1)S(1)} %get-tuple-element.62), channel_id=1, source_target_pairs={{0,15},{1,14},{2,13},{3,12},{4,11},{5,10},{6,9},{7,8},{8,7},{9,6},... | collective-permute-start | bytes 3080 | tf_op jit(solution)/shard_map/ppermute | solution.py:26
  82.7 1.8 %collective-permute-done.13 = bf16[2,8,32]{2,1,0:T(8,128)(2,1)S(1)} collective-permute-done((bf16[2,8,32]{2,1,0:T(8,128)(2,1)S(1)}, bf16[2,8,32]{2,1,0:T(8,128)(2,1)S(1)}, u32[]{:S(2)}, u32[]{:S(2)}) %collective-permute-start.13) | collective-permute-done | bytes 1056 | tf_op jit(solution)/shard_map/ppermute | solution.py:26
  84.8 0.6 copy-done.5
  85.4 0.9 %fusion.35 = bf16[2,32,128]{2,1,0:T(8,128)(2,1)} fusion(f32[2,32,128]{2,1,0:T(8,128)S(1)} %reshape.143, bf16[2,32,128]{2,1,0:T(8,128)(2,1)S(1)} %fusion.33, bf16[128,128]{1,0:T(8,128)(2,1)S(1)} %copy-done.5, bf16[128,128]{1,0:T(8,128)(2,1)S(1)} %copy-done.6, f32[2,32]{1,0:T(2,128)S(1)} %add_rsqrt_fusion, f32[2,32]{1,0:T(2,128)S(1)} %broadcast_multiply_fusion.1), kind=kOutput, calls=%fused_computation.40 | convolution fusion | flops 4292608 | bytes 131584 | tf_op jit(solution)/shard_map/rjf,fc->rjc/dot_general | solution.py:135
  (87 shorter events, 2.8 us)
Async XLA Ops:
  0.0 1.1 %copy-start = (bf16[128,512]{1,0:T(8,128)(2,1)S(1)}, bf16[128,512]{1,0:T(8,128)(2,1)}, u32[]{:S(2)}) copy-start(bf16[128,512]{1,0:T(8,128)(2,1)} %param.13) | copy-start | bytes 393220
  0.0 0.9 copy-start.1
  2.3 13.9 %all-to-all-start = ((bf16[16,2,256]{2,1,0:T(2,128)(2,1)}), bf16[16,2,256]{2,1,0:T(2,128)(2,1)S(1)}, u32[]{:S(2)}, u32[]{:S(2)}) async-start(bf16[16,2,256]{2,1,0:T(2,128)(2,1)} %reshape.156), calls=%async_computation | async-start | bytes 32768 | tf_op jit(solution)/shard_map/all_to_all | solution.py:89
  10.5 9.1 %copy-start.3 = (bf16[128,128]{1,0:T(8,128)(2,1)S(1)}, bf16[128,128]{1,0:T(8,128)(2,1)}, u32[]{:S(2)}) copy-start(bf16[128,128]{1,0:T(8,128)(2,1)} %param.14) | copy-start | bytes 98308
  16.2 9.9 %all-to-all-start.1 = ((bf16[16,2,256]{2,1,0:T(2,128)(2,1)}), bf16[16,2,256]{2,1,0:T(2,128)(2,1)S(1)}, u32[]{:S(2)}, u32[]{:S(2)}) async-start(bf16[16,2,256]{2,1,0:T(2,128)(2,1)} %reshape.158), calls=%async_computation.1 | async-start | bytes 32768 | tf_op jit(solution)/shard_map/all_to_all | solution.py:90
  27.2 3.6 %copy-start.8 = (s32[32]{0:T(128)S(1)}, s32[32]{0:T(128)}, u32[]{:S(2)}) copy-start(s32[32]{0:T(128)} %param.12) | copy-start | bytes 388
  27.2 10.1 %all-to-all-start.2 = ((bf16[16,2,256]{2,1,0:T(2,128)(2,1)}), bf16[16,2,256]{2,1,0:T(2,128)(2,1)S(1)}, u32[]{:S(2)}, u32[]{:S(2)}) async-start(bf16[16,2,256]{2,1,0:T(2,128)(2,1)} %reshape.160), calls=%async_computation.2 | async-start | bytes 32768 | tf_op jit(solution)/shard_map/all_to_all | solution.py:95
  30.9 0.9 %copy-start.2 = (bf16[128,384]{1,0:T(8,128)(2,1)S(1)}, bf16[128,384]{1,0:T(8,128)(2,1)}, u32[]{:S(2)}) copy-start(bf16[128,384]{1,0:T(8,128)(2,1)} %param.16) | copy-start | bytes 294916
  37.5 0.8 copy-start.4
  39.8 3.6 %copy-start.7 = (bf16[128,4]{0,1:T(4,128)(2,1)S(1)}, bf16[128,4]{0,1:T(4,128)(2,1)}, u32[]{:S(2)}) copy-start(bf16[128,4]{0,1:T(4,128)(2,1)} %param.17) | copy-start | bytes 3076
  39.8 10.4 %all-to-all-start.3 = ((bf16[16,2,3,256]{3,1,2,0:T(2,128)(2,1)}), bf16[16,2,3,256]{3,1,2,0:T(2,128)(2,1)S(1)}, u32[]{:S(2)}, u32[]{:S(2)}) async-start(bf16[16,2,3,256]{3,1,2,0:T(2,128)(2,1)} %reshape.155), calls=%async_computation.3 | async-start | bytes 98304 | tf_op jit(solution)/shard_map/all_to_all | solution.py:120
  50.8 10.0 %all-to-all-start.4 = ((f32[16,2,32]{2,1,0:T(2,128)}), f32[16,2,32]{2,1,0:T(2,128)S(1)}, u32[]{:S(2)}, u32[]{:S(2)}) async-start(f32[16,2,32]{2,1,0:T(2,128)} %bitcast.36), calls=%async_computation.4 | async-start | bytes 32768 | tf_op jit(solution)/shard_map/all_to_all | solution.py:122
  62.0 3.7 %collective-permute-start = (bf16[2,8,32]{2,1,0:T(8,128)(2,1)S(1)}, bf16[2,8,32]{2,1,0:T(8,128)(2,1)S(1)}, u32[]{:S(2)}, u32[]{:S(2)}) collective-permute-start(bf16[2,8,32]{2,1,0:T(8,128)(2,1)S(1)} %get-tuple-element.76), channel_id=1, source_target_pairs={{0,1},{1,0},{2,3},{3,2},{4,5},{5,4},{6,7},{7,6},{8,9},{9,8},{10,11... | collective-permute-start | bytes 3080 | tf_op jit(solution)/shard_map/ppermute | solution.py:26
  62.1 4.0 %collective-permute-start.1 = (bf16[2,8,32]{2,1,0:T(8,128)(2,1)S(1)}, bf16[2,8,32]{2,1,0:T(8,128)(2,1)S(1)}, u32[]{:S(2)}, u32[]{:S(2)}) collective-permute-start(bf16[2,8,32]{2,1,0:T(8,128)(2,1)S(1)} %get-tuple-element.75), channel_id=1, source_target_pairs={{0,2},{1,3},{2,0},{3,1},{4,6},{5,7},{6,4},{7,5},{8,10},{9,11},{10,... | collective-permute-start | bytes 3080 | tf_op jit(solution)/shard_map/ppermute | solution.py:26
  62.7 5.7 %collective-permute-start.2 = (bf16[2,8,32]{2,1,0:T(8,128)(2,1)S(1)}, bf16[2,8,32]{2,1,0:T(8,128)(2,1)S(1)}, u32[]{:S(2)}, u32[]{:S(2)}) collective-permute-start(bf16[2,8,32]{2,1,0:T(8,128)(2,1)S(1)} %get-tuple-element.74), channel_id=1, source_target_pairs={{0,3},{1,2},{2,1},{3,0},{4,7},{5,6},{6,5},{7,4},{8,11},{9,10},{10,... | collective-permute-start | bytes 3080 | tf_op jit(solution)/shard_map/ppermute | solution.py:26
  63.9 4.9 %collective-permute-start.3 = (bf16[2,8,32]{2,1,0:T(8,128)(2,1)S(1)}, bf16[2,8,32]{2,1,0:T(8,128)(2,1)S(1)}, u32[]{:S(2)}, u32[]{:S(2)}) collective-permute-start(bf16[2,8,32]{2,1,0:T(8,128)(2,1)S(1)} %get-tuple-element.73), channel_id=1, source_target_pairs={{0,4},{1,5},{2,6},{3,7},{4,0},{5,1},{6,2},{7,3},{8,12},{9,13},{10,... | collective-permute-start | bytes 3080 | tf_op jit(solution)/shard_map/ppermute | solution.py:26
  64.4 6.7 %collective-permute-start.4 = (bf16[2,8,32]{2,1,0:T(8,128)(2,1)S(1)}, bf16[2,8,32]{2,1,0:T(8,128)(2,1)S(1)}, u32[]{:S(2)}, u32[]{:S(2)}) collective-permute-start(bf16[2,8,32]{2,1,0:T(8,128)(2,1)S(1)} %get-tuple-element.72), channel_id=1, source_target_pairs={{0,5},{1,4},{2,7},{3,6},{4,1},{5,0},{6,3},{7,2},{8,13},{9,12},{10,... | collective-permute-start | bytes 3080 | tf_op jit(solution)/shard_map/ppermute | solution.py:26
  65.7 5.8 %collective-permute-start.5 = (bf16[2,8,32]{2,1,0:T(8,128)(2,1)S(1)}, bf16[2,8,32]{2,1,0:T(8,128)(2,1)S(1)}, u32[]{:S(2)}, u32[]{:S(2)}) collective-permute-start(bf16[2,8,32]{2,1,0:T(8,128)(2,1)S(1)} %get-tuple-element.71), channel_id=1, source_target_pairs={{0,6},{1,7},{2,4},{3,5},{4,2},{5,3},{6,0},{7,1},{8,14},{9,15},{10,... | collective-permute-start | bytes 3080 | tf_op jit(solution)/shard_map/ppermute | solution.py:26
  66.2 8.4 %collective-permute-start.6 = (bf16[2,8,32]{2,1,0:T(8,128)(2,1)S(1)}, bf16[2,8,32]{2,1,0:T(8,128)(2,1)S(1)}, u32[]{:S(2)}, u32[]{:S(2)}) collective-permute-start(bf16[2,8,32]{2,1,0:T(8,128)(2,1)S(1)} %get-tuple-element.70), channel_id=1, source_target_pairs={{0,7},{1,6},{2,5},{3,4},{4,3},{5,2},{6,1},{7,0},{8,15},{9,14},{10,... | collective-permute-start | bytes 3080 | tf_op jit(solution)/shard_map/ppermute | solution.py:26
  68.3 6.7 %collective-permute-start.7 = (bf16[2,8,32]{2,1,0:T(8,128)(2,1)S(1)}, bf16[2,8,32]{2,1,0:T(8,128)(2,1)S(1)}, u32[]{:S(2)}, u32[]{:S(2)}) collective-permute-start(bf16[2,8,32]{2,1,0:T(8,128)(2,1)S(1)} %get-tuple-element.69), channel_id=1, source_target_pairs={{0,8},{1,9},{2,10},{3,11},{4,12},{5,13},{6,14},{7,15},{8,0},{9,1},... | collective-permute-start | bytes 3080 | tf_op jit(solution)/shard_map/ppermute | solution.py:26
  68.8 9.3 %collective-permute-start.8 = (bf16[2,8,32]{2,1,0:T(8,128)(2,1)S(1)}, bf16[2,8,32]{2,1,0:T(8,128)(2,1)S(1)}, u32[]{:S(2)}, u32[]{:S(2)}) collective-permute-start(bf16[2,8,32]{2,1,0:T(8,128)(2,1)S(1)} %get-tuple-element.68), channel_id=1, source_target_pairs={{0,9},{1,8},{2,11},{3,10},{4,13},{5,12},{6,15},{7,14},{8,1},{9,0},... | collective-permute-start | bytes 3080 | tf_op jit(solution)/shard_map/ppermute | solution.py:26
  71.0 7.6 %collective-permute-start.9 = (bf16[2,8,32]{2,1,0:T(8,128)(2,1)S(1)}, bf16[2,8,32]{2,1,0:T(8,128)(2,1)S(1)}, u32[]{:S(2)}, u32[]{:S(2)}) collective-permute-start(bf16[2,8,32]{2,1,0:T(8,128)(2,1)S(1)} %get-tuple-element.67), channel_id=1, source_target_pairs={{0,10},{1,11},{2,8},{3,9},{4,14},{5,15},{6,12},{7,13},{8,2},{9,3},... | collective-permute-start | bytes 3080 | tf_op jit(solution)/shard_map/ppermute | solution.py:26
  71.5 11.1 %collective-permute-start.10 = (bf16[2,8,32]{2,1,0:T(8,128)(2,1)S(1)}, bf16[2,8,32]{2,1,0:T(8,128)(2,1)S(1)}, u32[]{:S(2)}, u32[]{:S(2)}) collective-permute-start(bf16[2,8,32]{2,1,0:T(8,128)(2,1)S(1)} %get-tuple-element.66), channel_id=1, source_target_pairs={{0,11},{1,10},{2,9},{3,8},{4,15},{5,14},{6,13},{7,12},{8,3},{9,2},... | collective-permute-start | bytes 3080 | tf_op jit(solution)/shard_map/ppermute | solution.py:26
  74.6 8.0 %collective-permute-start.11 = (bf16[2,8,32]{2,1,0:T(8,128)(2,1)S(1)}, bf16[2,8,32]{2,1,0:T(8,128)(2,1)S(1)}, u32[]{:S(2)}, u32[]{:S(2)}) collective-permute-start(bf16[2,8,32]{2,1,0:T(8,128)(2,1)S(1)} %get-tuple-element.65), channel_id=1, source_target_pairs={{0,12},{1,13},{2,14},{3,15},{4,8},{5,9},{6,10},{7,11},{8,4},{9,5},... | collective-permute-start | bytes 3080 | tf_op jit(solution)/shard_map/ppermute | solution.py:26
  75.1 7.6 %collective-permute-start.12 = (bf16[2,8,32]{2,1,0:T(8,128)(2,1)S(1)}, bf16[2,8,32]{2,1,0:T(8,128)(2,1)S(1)}, u32[]{:S(2)}, u32[]{:S(2)}) collective-permute-start(bf16[2,8,32]{2,1,0:T(8,128)(2,1)S(1)} %get-tuple-element.64), channel_id=1, source_target_pairs={{0,13},{1,12},{2,15},{3,14},{4,9},{5,8},{6,11},{7,10},{8,5},{9,4},... | collective-permute-start | bytes 3080 | tf_op jit(solution)/shard_map/ppermute | solution.py:26
  78.2 6.3 %collective-permute-start.13 = (bf16[2,8,32]{2,1,0:T(8,128)(2,1)S(1)}, bf16[2,8,32]{2,1,0:T(8,128)(2,1)S(1)}, u32[]{:S(2)}, u32[]{:S(2)}) collective-permute-start(bf16[2,8,32]{2,1,0:T(8,128)(2,1)S(1)} %get-tuple-element.63), channel_id=1, source_target_pairs={{0,14},{1,15},{2,12},{3,13},{4,10},{5,11},{6,8},{7,9},{8,6},{9,7},... | collective-permute-start | bytes 3080 | tf_op jit(solution)/shard_map/ppermute | solution.py:26
  78.7 5.8 %collective-permute-start.14 = (bf16[2,8,32]{2,1,0:T(8,128)(2,1)S(1)}, bf16[2,8,32]{2,1,0:T(8,128)(2,1)S(1)}, u32[]{:S(2)}, u32[]{:S(2)}) collective-permute-start(bf16[2,8,32]{2,1,0:T(8,128)(2,1)S(1)} %get-tuple-element.62), channel_id=1, source_target_pairs={{0,15},{1,14},{2,13},{3,12},{4,11},{5,10},{6,9},{7,8},{8,7},{9,6},... | collective-permute-start | bytes 3080 | tf_op jit(solution)/shard_map/ppermute | solution.py:26
  84.6 0.8 copy-start.5
  84.6 0.8 copy-start.6
